TPU v7x, 32 devices: a whole 2x2x4 slice. The times are simulated.
32 devices in a mesh: row: 4 (over y, x), col: 8 (over z, core).
Axes of the slice: x: 2, y: 2, z: 4, core: 2. Of those that a mesh axis runs over, the one named last changes fastest.
Arguments:
- operator: float32 [4096, 4096], P('row', 'col'), may hold values from -0.09375 to 0.09375
- state: float32 [4096, 4096], P('row', 'col'), may hold values from -60 to 60, as said below
- source: float32 [4096, 4096], P('row', 'col'), may hold values from -60 to 60, as said below
Outputs:
- state_next: float32 [4096, 4096], P('row', 'col')
- operator_fourth: float32 [4096, 4096], P('row', 'col')
Inputs may be any that keep to these rules, and one draw needn't show every extreme that they name: symmetric: state equals its transpose. symmetric: source equals its transpose.
All inputs are finite; a program needn't handle non-finite values.
Results may differ from a plain program's by a relative error of at most 0.000098.
Values sent between devices are 32-bit elements; how exact they have to be, the bound alone decides.
No kernel may reach another device: no remote copies, remote signals or barrier semaphores. Data moves between devices by JAX's collectives and lax.ppermute only.
A program may use at most 128 MiB of HBM per device.

v0:
```python
import jax
import jax.numpy as jnp
from jax import lax
from jax.sharding import PartitionSpec as P


def matmul(left, right):
    return jnp.dot(left, right, preferred_element_type=jnp.float32, precision=lax.Precision.HIGHEST)


def split_pieces(block, groups):
    rows, columns = block.shape
    width = columns // groups
    pieces = block.reshape(2, columns, groups, width).transpose(2, 0, 3, 1)
    return pieces.reshape(2 * groups, width, columns)


def join_pieces(pieces, groups):
    count, width, columns = pieces.shape
    joined = pieces.reshape(groups, 2, width, columns).transpose(1, 0, 2, 3)
    return joined.reshape(2 * groups * width, columns)


def folder(panel, piece):
    return matmul(panel, piece)


def on_device(operator, state, source):
    groups = lax.axis_size("row")
    row_panel = lax.all_gather(operator, "col", axis=1, tiled=True)
    product = matmul(row_panel, lax.all_gather(state, "row", axis=0, tiled=True))
    square = matmul(row_panel, lax.all_gather(operator, "row", axis=0, tiled=True))
    moved = lax.all_to_all(
        lax.all_to_all(
            split_pieces(product, groups), "row", split_axis=0, concat_axis=0, tiled=True
        ),
        "col",
        split_axis=0,
        concat_axis=0,
        tiled=True,
    )
    turned = join_pieces(
        lax.all_to_all(moved, "row", split_axis=0, concat_axis=0, tiled=True), groups
    )
    state_next = folder(row_panel, lax.all_gather(turned, "row", axis=0, tiled=True)) + source
    square_panel = lax.all_gather(square, "col", axis=1, tiled=True)
    operator_fourth = folder(square_panel, lax.all_gather(square, "row", axis=0, tiled=True))
    return (state_next, operator_fourth)


def solution(mesh):
    in_specs = (P("row", "col"), P("row", "col"), P("row", "col"))
    out_specs = (P("row", "col"), P("row", "col"))
    return jax.shard_map(
        on_device, mesh=mesh, in_specs=in_specs, out_specs=out_specs, check_vma=False
    )
```

profile of v0, /device:TPU:0, one launch (start us, length us, event | category | flops | bytes accessed | tf_op | source)
XLA Modules:
  0.0 784.8 jit_solution(5429908569219231628)
XLA Ops:
  7.2 0.7 all-gather.9.cloned.1.call-update
  7.9 0.7 all-gather.7.cloned.1.call-update
  8.7 0.7 all-gather.13.cloned.1.call-update
  9.4 0.0 all-gather.11.cloned.1.call-start
  9.4 90.6 %all-gather.9.cloned.1.call-done = f32[4096,512]{1,0:T(8,128)} async-done(((f32[1024,512]{1,0:T(8,128)}), f32[4096,512]{1,0:T(8,128)}) %all-gather.9.cloned.1.call-update) | async-done | bytes 8388624 | tf_op jit(solution)/shard_map/all_gather | solution.py:31
  100.1 152.7 %all-gather.7.cloned.1.call-done = f32[1024,4096]{1,0:T(8,128)} async-done(((f32[1024,512]{1,0:T(8,128)}), f32[1024,4096]{1,0:T(8,128)}) %all-gather.7.cloned.1.call-update) | async-done | bytes 16777232 | tf_op jit(solution)/shard_map/all_gather | solution.py:30
  252.8 31.0 %fusion = f32[1024,512]{1,0:T(8,128)} fusion(f32[1024,4096]{1,0:T(8,128)} %all-gather.7.cloned.1.call-done, f32[4096,512]{1,0:T(8,128)} %all-gather.9.cloned.1.call-done), kind=kOutput, calls=%fused_computation.1 | convolution fusion | flops 25769803776 | bytes 27262976 | tf_op jit(solution)/shard_map/dot_general | solution.py:8
  283.7 1.9 reshape.16
  285.7 1.8 copy.7
  287.5 51.3 %all_to_all.15 = f32[8,128,512]{2,1,0:T(8,128)S(1)} all-to-all(f32[8,128,512]{2,1,0:T(8,128)} %bitcast.18), channel_id=1, replica_groups=mesh['row'=4,'col'=8] {'row'}, dimensions={0} | all-to-all | bytes 4194304 | tf_op jit(solution)/shard_map/all_to_all | solution.py:34
  338.8 51.5 %all_to_all.16 = f32[8,128,512]{2,1,0:T(8,128)S(1)} all-to-all(f32[8,128,512]{2,1,0:T(8,128)S(1)} %all_to_all.15), channel_id=1, replica_groups=mesh['row'=4,'col'=8] {'col'}, dimensions={0} | all-to-all | bytes 4194304 | tf_op jit(solution)/shard_map/all_to_all | solution.py:33
  390.3 27.7 %all_to_all.17 = f32[8,128,512]{2,1,0:T(8,128)S(1)} all-to-all(f32[8,128,512]{2,1,0:T(8,128)S(1)} %all_to_all.16), channel_id=1, replica_groups=mesh['row'=4,'col'=8] {'row'}, dimensions={0} | all-to-all | bytes 4194304 | tf_op jit(solution)/shard_map/all_to_all | solution.py:43
  418.0 1.6 copy.8
  419.6 0.2 all-gather.17.cloned.1.call-start
  419.9 31.1 %fusion.1 = f32[1024,512]{1,0:T(8,128)} fusion(f32[1024,4096]{1,0:T(8,128)} %all-gather.7.cloned.1.call-done, f32[4096,512]{1,0:T(8,128)} %all-gather.13.cloned.1.call-done), kind=kOutput, calls=%fused_computation.2 | convolution fusion | flops 25769803776 | bytes 27262976 | tf_op jit(solution)/shard_map/dot_general | solution.py:8
  451.0 0.0 all-gather.15.cloned.1.call-start
  451.0 0.5 all-gather.15.cloned.1.call-update
  451.6 1.8 copy.9
  453.4 51.8 %all-gather.11.cloned.1.call-done = f32[4096,512]{1,0:T(8,128)} async-done(((f32[1024,512]{1,0:T(8,128)}), f32[4096,512]{1,0:T(8,128)}) %all-gather.11.cloned.1.call-update) | async-done | bytes 8388624 | tf_op jit(solution)/shard_map/all_gather | solution.py:45
  505.2 56.7 %bitcast_add_fusion = f32[1024,512]{0,1:T(8,128)S(1)} fusion(f32[1024,512]{0,1:T(8,128)} %copy.9, f32[4096,512]{1,0:T(8,128)} %all-gather.11.cloned.1.call-done, f32[1024,4096]{1,0:T(8,128)} %all-gather.7.cloned.1.call-done), kind=kOutput, calls=%fused_computation | convolution fusion | flops 25770328064 | bytes 29360128 | tf_op jit(solution)/shard_map/dot_general | solution.py:8
  562.0 1.8 copy.10
  563.8 30.6 %all-gather.17.cloned.1.call-done = f32[4096,512]{1,0:T(8,128)} async-done(((f32[1024,512]{1,0:T(8,128)}), f32[4096,512]{1,0:T(8,128)}) %all-gather.17.cloned.1.call-update) | async-done | bytes 8388624 | tf_op jit(solution)/shard_map/all_gather | solution.py:47
  594.4 152.6 %all-gather.15.cloned.1.call-done = f32[1024,4096]{1,0:T(8,128)} async-done(((f32[1024,512]{1,0:T(8,128)}), f32[1024,4096]{1,0:T(8,128)}) %all-gather.15.cloned.1.call-update) | async-done | bytes 16777232 | tf_op jit(solution)/shard_map/all_gather | solution.py:46
  747.0 31.0 %fusion.2 = f32[1024,512]{1,0:T(8,128)} fusion(f32[1024,4096]{1,0:T(8,128)} %all-gather.15.cloned.1.call-done, f32[4096,512]{1,0:T(8,128)} %all-gather.17.cloned.1.call-done), kind=kOutput, calls=%fused_computation.3 | convolution fusion | flops 25769803776 | bytes 27262976 | tf_op jit(solution)/shard_map/dot_general | solution.py:8
  (8 shorter events, 0.2 us)
Async XLA Ops:
  7.2 92.9 %all-gather.9.cloned.1.call-start = ((), (), s32[]{:S(2)}) async-start(), calls=%async_computation.4 | async-start | bytes 10485760 | tf_op jit(solution)/shard_map/all_gather | solution.py:31
  7.9 244.9 %all-gather.7.cloned.1.call-start = ((), (), s32[]{:S(2)}) async-start(), calls=%async_computation.3 | async-start | bytes 18874368 | tf_op jit(solution)/shard_map/all_gather | solution.py:30
  8.6 411.2 %all-gather.13.cloned.1.call-start = ((), (), s32[]{:S(2)}) async-start(), calls=%async_computation.6 | async-start | bytes 10485760 | tf_op jit(solution)/shard_map/all_gather | solution.py:32
  9.4 495.9 %all-gather.11.cloned.1.call-start = ((), (), s32[]{:S(2)}) async-start(), calls=%async_computation.5 | async-start | bytes 10485760 | tf_op jit(solution)/shard_map/all_gather | solution.py:45
  419.6 32.0 %copy-start = (f32[1024,512]{1,0:T(8,128)S(1)}, f32[1024,512]{1,0:T(8,128)}, u32[]{:S(2)}) copy-start(f32[1024,512]{1,0:T(8,128)} %param.5) | copy-start | bytes 6291460
  419.6 174.8 %all-gather.17.cloned.1.call-start = ((), (), s32[]{:S(2)}) async-start(), calls=%async_computation.8 | async-start | bytes 10485760 | tf_op jit(solution)/shard_map/all_gather | solution.py:47
  451.0 296.0 %all-gather.15.cloned.1.call-start = ((), (), s32[]{:S(2)}) async-start(), calls=%async_computation.7 | async-start | bytes 18874368 | tf_op jit(solution)/shard_map/all_gather | solution.py:46
Sparse Core Ops, SparseCore 0:
  9.8 90.1 all-gather.8
  101.7 151.0 all-gather.6
  254.6 107.1 all-gather.12
  419.7 85.4 all-gather.10
  506.9 87.4 all-gather.16
  595.9 151.0 all-gather.14
where the time goes:
time: 785 us
  waiting for transfers between devices  481 us (61%)
  matrix products  150 us (19%)
  blocking collectives  131 us (17%)
  between operations  14.2 us (2%)
  local copies, waits for them, and re-layouts  8.94 us (1%)
    all_gather x1, waiting for transfers between devices, on_device(): row_panel = lax.all_gather(operator, 'col', axis=1, tiled=True)  153 us
    all_gather x1, waiting for transfers between devices, on_device(): square_panel = lax.all_gather(square, 'col', axis=1, tiled=True)  153 us
    dot_general x4, matrix products, matmul(): jnp.dot(left, right, preferred_element_type=jnp.float32, precision=lax.Pr...  150 us
    all_gather x1, waiting for transfers between devices, on_device(): lax.all_gather(state, 'row', axis=0, tiled=True)  90.6 us
    all_gather x1, waiting for transfers between devices, on_device(): lax.all_gather(turned, 'row', axis=0, tiled=True)  51.8 us
    all_to_all x1, blocking collectives, on_device(): lax.all_to_all(lax.all_to_all(split_pieces(product, groups), 'row', split...  51.5 us
    all_to_all x1, blocking collectives, on_device(): lax.all_to_all(split_pieces(product, groups), 'row', split_axis=0, concat...  51.3 us
    all_gather x1, waiting for transfers between devices, on_device(): lax.all_gather(square, 'row', axis=0, tiled=True)  30.6 us
  transfers between devices with their start and end apart: 6, of which 5 were waited for; matrix products, arithmetic and copies ran while one was open for 16% of the time, Pallas kernels for 0%

commit v1 on v0

--- a/solution.py
+++ b/solution.py
@@ -27,7 +27,7 @@
 
 def on_device(operator, state, source):
     groups = lax.axis_size("row")
-    row_panel = lax.all_gather(operator, "col", axis=1, tiled=True)
+    row_panel = jnp.concatenate(lax.all_gather(operator, "col"), axis=1)
     product = matmul(row_panel, lax.all_gather(state, "row", axis=0, tiled=True))
     square = matmul(row_panel, lax.all_gather(operator, "row", axis=0, tiled=True))
     moved = lax.all_to_all(

time: 785 us -> 834 us (1.062); the launches traced: 785 us -> 825 us
  local copies, waits for them, and re-layouts: 8.94 us -> 65.1 us
  waiting for transfers between devices: 481 us -> 460 us
    dot_general x0 -> x2, local copies, waits for them, and re-layouts: none -> 27.2 us  [matmul(): jnp.dot(left, right, preferred_element_type=jnp.float32, precision=lax.Pr...]
    all_gather x0 -> x1, local copies, waits for them, and re-layouts: none -> 18.3 us  [on_device(): row_panel = jnp.concatenate(lax.all_gather(operator, 'col'), axis=1)]
    all_to_all x1, blocking collectives: 51.5 us -> 66.8 us  [on_device(): lax.all_to_all(lax.all_to_all(split_pieces(product, groups), 'row', split...]
    unnamed x4 -> x5, local copies, waits for them, and re-layouts: 3.63 us -> 16.2 us
    all_gather x1, waiting for transfers between devices: 51.8 us -> 39.4 us  [on_device(): lax.all_gather(turned, 'row', axis=0, tiled=True)]
    all_to_all x1, blocking collectives: 51.3 us -> 40.8 us  [on_device(): lax.all_to_all(split_pieces(product, groups), 'row', split_axis=0, concat...]
    all_gather x1, waiting for transfers between devices: 153 us -> 144 us  [on_device(): row_panel = jnp.concatenate(lax.all_gather(operator, 'col'), axis=1)]
  transfers between devices with their start and end apart: 6 -> 6, of which waited for: 5 -> 5; matrix products, arithmetic and copies ran while one was open for 16% -> 22% of each run, Pallas kernels for 0% -> 0%
where the time goes in v1:
time: 834 us; the launch traced here: 825 us
  waiting for transfers between devices  460 us (55%)
  matrix products  150 us (18%)
  blocking collectives  135 us (16%)
  local copies, waits for them, and re-layouts  65.1 us (8%)
  between operations  14.5 us (2%)
    all_gather x1, waiting for transfers between devices, on_device(): square_panel = lax.all_gather(square, 'col', axis=1, tiled=True)  153 us
    dot_general x4, matrix products, matmul(): jnp.dot(left, right, preferred_element_type=jnp.float32, precision=lax.Pr...  150 us
    all_gather x1, waiting for transfers between devices, on_device(): row_panel = jnp.concatenate(lax.all_gather(operator, 'col'), axis=1)  144 us
    all_gather x1, waiting for transfers between devices, on_device(): lax.all_gather(state, 'row', axis=0, tiled=True)  90.6 us
    all_to_all x1, blocking collectives, on_device(): lax.all_to_all(lax.all_to_all(split_pieces(product, groups), 'row', split...  66.8 us
    all_to_all x1, blocking collectives, on_device(): lax.all_to_all(split_pieces(product, groups), 'row', split_axis=0, concat...  40.8 us
    all_gather x1, waiting for transfers between devices, on_device(): lax.all_gather(turned, 'row', axis=0, tiled=True)  39.4 us
    all_gather x1, waiting for transfers between devices, on_device(): lax.all_gather(square, 'row', axis=0, tiled=True)  30.7 us
  transfers between devices with their start and end apart: 6, of which 5 were waited for; matrix products, arithmetic and copies ran while one was open for 22% of the time, Pallas kernels for 0%

profile of v1, /device:TPU:0, one launch (start us, length us, event | category | flops | bytes accessed | tf_op | source)
XLA Modules:
  0.0 824.7 jit_solution(14138794523996968435)
XLA Ops:
  7.2 0.7 all-gather.8.cloned.1.call-update
  7.9 0.7 all-gather.18.cloned.1.call-update
  8.7 0.7 all-gather.12.cloned.1.call-update
  9.4 90.6 %all-gather.8.cloned.1.call-done = f32[4096,512]{1,0:T(8,128)} async-done(((f32[1024,512]{1,0:T(8,128)}), f32[4096,512]{1,0:T(8,128)}) %all-gather.8.cloned.1.call-update) | async-done | bytes 8388624 | tf_op jit(solution)/shard_map/all_gather | solution.py:31
  100.1 8.9 %copy.10 = f32[512,4096]{1,0:T(8,128)} copy(f32[512,4096]{0,1:T(8,128)} %bitcast.38) | data formatting | bytes 16777216 | tf_op jit(solution)/shard_map/dot_general | solution.py:8
  109.0 143.8 %all-gather.18.cloned.1.call-done = f32[8192,512]{1,0:T(8,128)} async-done(((f32[1024,512]{1,0:T(8,128)}), f32[8192,512]{1,0:T(8,128)}) %all-gather.18.cloned.1.call-update) | async-done | bytes 16777232 | tf_op jit(solution)/shard_map/all_gather | solution.py:30
  252.8 18.3 %copy.19 = f32[8,1024,512]{2,0,1:T(8,128)} copy(f32[8,1024,512]{2,1,0:T(8,128)} %bitcast.33) | data formatting | bytes 33554432 | tf_op jit(solution)/shard_map/all_gather | solution.py:30
  271.0 18.2 %reshape.29 = f32[2,512,4096,1]{2,1,0,3:T(8,128)} reshape(f32[1024,8,512]{2,1,0:T(8,128)} %bitcast.35) | data formatting | bytes 33554432 | tf_op jit(solution)/shard_map/dot_general | solution.py:8
  289.3 31.0 %fusion.2 = f32[4,2,128,512]{2,3,0,1:T(8,128)} fusion(f32[4,128,4096,1]{2,1,0,3:T(8,128)} %bitcast.39, f32[2,512,4096,1]{2,1,0,3:T(8,128)} %reshape.29), kind=kOutput, calls=%fused_computation.3 | convolution fusion | flops 25769803776 | bytes 27262976 | tf_op jit(solution)/shard_map/dot_general | solution.py:8
  320.3 1.9 copy.11
  322.2 40.8 %all_to_all.15 = f32[8,128,512]{2,1,0:T(8,128)S(1)} all-to-all(f32[8,128,512]{2,1,0:T(8,128)S(1)} %bitcast.41), channel_id=1, replica_groups=mesh['row'=4,'col'=8] {'row'}, dimensions={0} | all-to-all | bytes 4194304 | tf_op jit(solution)/shard_map/all_to_all | solution.py:34
  363.0 66.8 %all_to_all.16 = f32[8,128,512]{2,1,0:T(8,128)S(1)} all-to-all(f32[8,128,512]{2,1,0:T(8,128)S(1)} %all_to_all.15), channel_id=1, replica_groups=mesh['row'=4,'col'=8] {'col'}, dimensions={0} | all-to-all | bytes 4194304 | tf_op jit(solution)/shard_map/all_to_all | solution.py:33
  429.8 27.7 %all_to_all.17 = f32[8,128,512]{2,1,0:T(8,128)S(1)} all-to-all(f32[8,128,512]{2,1,0:T(8,128)S(1)} %all_to_all.16), channel_id=1, replica_groups=mesh['row'=4,'col'=8] {'row'}, dimensions={0} | all-to-all | bytes 4194304 | tf_op jit(solution)/shard_map/all_to_all | solution.py:43
  457.5 1.6 copy.12
  459.1 12.5 %copy.16 = f32[128,8,8,512]{3,1,2,0:T(8,128)} copy(f32[128,8,8,512]{3,1,0,2:T(8,128)} %bitcast.34) | data formatting | bytes 33554432
  471.7 31.2 %fusion.5 = f32[1024,512]{1,0:T(8,128)} fusion(f32[1024,4096]{1,0:T(8,128)} %bitcast.36, f32[4096,512]{1,0:T(8,128)} %all-gather.12.cloned.1.call-done), kind=kOutput, calls=%fused_computation.5 | convolution fusion | flops 25769803776 | bytes 27262976 | tf_op jit(solution)/shard_map/dot_general | solution.py:8
  502.9 0.5 all-gather.14.cloned.1.call-update
  503.5 1.8 copy.13
  505.3 39.4 %all-gather.10.cloned.1.call-done = f32[4096,512]{1,0:T(8,128)} async-done(((f32[1024,512]{1,0:T(8,128)}), f32[4096,512]{1,0:T(8,128)}) %all-gather.10.cloned.1.call-update) | async-done | bytes 8388624 | tf_op jit(solution)/shard_map/all_gather | solution.py:45
  544.7 56.7 %bitcast_add_fusion = f32[1024,512]{0,1:T(8,128)S(1)} fusion(f32[1024,512]{0,1:T(8,128)} %copy.13, f32[4096,512]{1,0:T(8,128)} %all-gather.10.cloned.1.call-done, f32[1024,4096]{1,0:T(8,128)} %bitcast.37), kind=kOutput, calls=%fused_computation.2 | convolution fusion | flops 25770328064 | bytes 29360128 | tf_op jit(solution)/shard_map/dot_general | solution.py:8
  601.4 1.8 copy.14
  603.2 30.7 %all-gather.16.cloned.1.call-done = f32[4096,512]{1,0:T(8,128)} async-done(((f32[1024,512]{1,0:T(8,128)}), f32[4096,512]{1,0:T(8,128)}) %all-gather.16.cloned.1.call-update) | async-done | bytes 8388624 | tf_op jit(solution)/shard_map/all_gather | solution.py:47
  633.9 152.6 %all-gather.14.cloned.1.call-done = f32[1024,4096]{1,0:T(8,128)} async-done(((f32[1024,512]{1,0:T(8,128)}), f32[1024,4096]{1,0:T(8,128)}) %all-gather.14.cloned.1.call-update) | async-done | bytes 16777232 | tf_op jit(solution)/shard_map/all_gather | solution.py:46
  786.5 31.0 %fusion.6 = f32[1024,512]{1,0:T(8,128)} fusion(f32[1024,4096]{1,0:T(8,128)} %all-gather.14.cloned.1.call-done, f32[4096,512]{1,0:T(8,128)} %all-gather.16.cloned.1.call-done), kind=kOutput, calls=%fused_computation.6 | convolution fusion | flops 25769803776 | bytes 27262976 | tf_op jit(solution)/shard_map/dot_general | solution.py:8
  (11 shorter events, 0.3 us)
Async XLA Ops:
  7.2 92.9 %all-gather.8.cloned.1.call-start = ((), (), s32[]{:S(2)}) async-start(), calls=%async_computation.3 | async-start | bytes 10485760 | tf_op jit(solution)/shard_map/all_gather | solution.py:31
  7.9 244.9 %all-gather.18.cloned.1.call-start = ((), (), s32[]{:S(2)}) async-start(), calls=%async_computation.8 | async-start | bytes 18874368 | tf_op jit(solution)/shard_map/all_gather | solution.py:30
  8.6 463.0 %all-gather.12.cloned.1.call-start = ((), (), s32[]{:S(2)}) async-start(), calls=%async_computation.5 | async-start | bytes 10485760 | tf_op jit(solution)/shard_map/all_gather | solution.py:32
  9.4 535.3 %all-gather.10.cloned.1.call-start = ((), (), s32[]{:S(2)}) async-start(), calls=%async_computation.4 | async-start | bytes 10485760 | tf_op jit(solution)/shard_map/all_gather | solution.py:45
  459.1 174.8 %all-gather.16.cloned.1.call-start = ((), (), s32[]{:S(2)}) async-start(), calls=%async_computation.7 | async-start | bytes 10485760 | tf_op jit(solution)/shard_map/all_gather | solution.py:47
  471.7 31.8 %copy-start = (f32[1024,512]{1,0:T(8,128)S(1)}, f32[1024,512]{1,0:T(8,128)}, u32[]{:S(2)}) copy-start(f32[1024,512]{1,0:T(8,128)} %param.5) | copy-start | bytes 6291460
  502.9 283.6 %all-gather.14.cloned.1.call-start = ((), (), s32[]{:S(2)}) async-start(), calls=%async_computation.6 | async-start | bytes 18874368 | tf_op jit(solution)/shard_map/all_gather | solution.py:46
Sparse Core Ops, SparseCore 0:
  9.8 90.1 all-gather.7
  101.6 151.0 all-gather.17
  254.6 107.3 all-gather.11
  459.2 85.4 all-gather.9
  546.4 87.4 all-gather.15
  635.4 151.0 all-gather.13
